TPU v7x, 32 devices: a whole 2x2x4 slice. The times are simulated.
32 devices in a mesh: dp: 4 (over x, core), seq: 4 (over z), tensor: 2 (over y).
Axes of the slice: x: 2, y: 2, z: 4, core: 2. Of those that a mesh axis runs over, the one named last changes fastest.
Arguments:
- query_vectors: bfloat16 [896, 4096], P(('dp', 'seq'), 'tensor'), may hold values from -128 to 128
- key_vectors: bfloat16 [896, 2048], P(('dp', 'seq'), 'tensor'), may hold values from -6 to 6
- value_vectors: bfloat16 [896, 2048], P(('dp', 'seq'), 'tensor'), may hold values from -6 to 6
- out_weight: bfloat16 [4096, 3584], P(None, 'tensor'), may hold values from -0.09375 to 0.09375
- residual: bfloat16 [896, 3584], P(('dp', 'seq'), 'tensor'), may hold values from -64 to 64
- post_gain: float32 [3584], P('tensor'), may hold values from 0.1 to 1.9
- final_gain: float32 [3584], P('tensor'), may hold values from 0.1 to 1.9
- vocab_weight: bfloat16 [16000, 3584], P(('dp', 'seq', 'tensor')), may hold values from -4 to 4
- segment_ids: int32 [4, 224], P('dp', 'seq'), may hold values from 0 to 7, as said below
- doc_starts: int32 [4, 8], P('dp'), may hold values from 0 to 223, as said below
- doc_index: int32 [4, 8], P('dp'), may hold values from 0 to 31
- targets: int32 [4, 224], replicated, may hold values from 0 to 15999
Outputs:
- token_logprob: float32 [4, 224], P('dp', 'seq')
- doc_loglik: float32 [32], replicated
- doc_counts: float32 [32], replicated
Inputs may be any that keep to these rules, and one draw needn't show every extreme that they name: `segment_ids`: within each row the numbers never fall and every number 0 to 7 appears; segment s of a row begins at doc_starts[row, s]; each segment holds 1 to 168 positions. doc_starts[row, 0] = 0 and the starts rise strictly along each row.
All inputs are finite; a program needn't handle non-finite values.
Results may differ from a plain program's by a relative error of at most 0.00074.
Values may be sent and summed in bfloat16 or wider, within the bound.
A program may use at most 64 MiB of HBM per device.

v0:
```python
import jax
import jax.numpy as jnp
from jax import lax
from jax.sharding import PartitionSpec as P

D = 3584
HEAD_DIM = 256


ATTENTION_CAP = 50.0
LOGIT_CAP = 30.0
EPSILON = 1e-06


def local(
    query_vectors,
    key_vectors,
    value_vectors,
    out_weight,
    residual,
    post_gain,
    final_gain,
    vocab_weight,
    segment_ids,
    doc_starts,
    doc_index,
    targets,
):
    tok_rows = query_vectors.shape[0]
    seg_row = segment_ids[0]
    starts = doc_starts[0]
    seg_count = starts.shape[0]
    slot_ids = jnp.arange(seg_count, dtype=jnp.int32)
    positions = lax.axis_index("seq") * tok_rows + jnp.arange(tok_rows, dtype=jnp.int32)
    doc_first = jnp.sum(
        jnp.where(seg_row[:, None] == slot_ids[None, :], starts[None, :], 0), axis=1
    )
    local_groups = key_vectors.shape[1] // HEAD_DIM
    group_size = query_vectors.shape[1] // key_vectors.shape[1]
    query_heads = query_vectors.reshape(tok_rows, local_groups, group_size, HEAD_DIM)
    score_scale = HEAD_DIM ** (-0.5)
    key_block = lax.all_gather(key_vectors, "seq", axis=0, tiled=True)
    value_block = lax.all_gather(value_vectors, "seq", axis=0, tiled=True)
    row_count = key_block.shape[0]
    key_heads = key_block.reshape(row_count, local_groups, HEAD_DIM)
    value_heads = value_block.reshape(row_count, local_groups, HEAD_DIM)
    raw_scores = jnp.einsum(
        "ikgd,jkd->ikgj", query_heads, key_heads, preferred_element_type=jnp.float32
    )
    capped = ATTENTION_CAP * jnp.tanh(raw_scores * score_scale / ATTENTION_CAP)
    key_positions = jnp.arange(row_count, dtype=jnp.int32)
    visible = (key_positions[None, :] <= positions[:, None]) & (
        key_positions[None, :] >= doc_first[:, None]
    )
    weights = jnp.where(visible[:, None, None, :], jnp.exp(capped), 0.0)
    rounded = weights.astype(jnp.bfloat16)
    numerator = jnp.einsum(
        "ikgj,jkd->ikgd", rounded, value_heads, preferred_element_type=jnp.float32
    )
    denominator = jnp.sum(weights, axis=-1)
    numerator, denominator = (numerator, denominator)
    attended = (
        (numerator / denominator[..., None])
        .reshape(tok_rows, query_vectors.shape[1])
        .astype(jnp.bfloat16)
    )
    branch = jnp.dot(
        lax.all_gather(attended, "tensor", axis=1, tiled=True),
        out_weight,
        preferred_element_type=jnp.float32,
    )
    carried_in = residual.astype(jnp.float32)
    gained = post_gain[None, :] * branch
    sq_branch, sq_carried, cross_sum, sq_gained = lax.psum(
        (
            jnp.sum(branch * branch, axis=1),
            jnp.sum(carried_in * carried_in, axis=1),
            jnp.sum(carried_in * gained, axis=1),
            jnp.sum(gained * gained, axis=1),
        ),
        "tensor",
    )
    inv_branch = 1.0 / jnp.sqrt(sq_branch / D + EPSILON)
    updated = carried_in + gained * inv_branch[:, None]
    sq_total = sq_carried + 2.0 * inv_branch * cross_sum + inv_branch * inv_branch * sq_gained
    hidden = (final_gain[None, :] * updated / jnp.sqrt(sq_total / D + EPSILON)[:, None]).astype(
        jnp.bfloat16
    )
    vocab_count = vocab_weight.shape[0]
    tensor_size = lax.axis_size("tensor")
    seq_size = lax.axis_size("seq")
    labels = targets.reshape(-1)
    flat_index = (
        lax.axis_index("dp") * seq_size + lax.axis_index("seq")
    ) * tensor_size + lax.axis_index("tensor")
    vocab_ids = flat_index * vocab_count + jnp.arange(vocab_count, dtype=jnp.int32)
    features = lax.all_gather(hidden, "tensor", axis=1, tiled=True)
    block_in = lax.all_gather(features, ("dp", "seq"), axis=0, tiled=True)
    logits = lax.dot_general(
        vocab_weight, block_in, (((1,), (1,)), ((), ())), preferred_element_type=jnp.float32
    )
    capped = LOGIT_CAP * jnp.tanh(logits / LOGIT_CAP)
    totals = jnp.sum(jnp.exp(capped), axis=0)
    chosen = jnp.sum(jnp.where(vocab_ids[:, None] == labels[None, :], capped, 0.0), axis=0)
    partial_value = jnp.stack([totals, chosen])
    totals, chosen = (
        lax.psum_scatter(
            partial_value[0], ("dp", "seq", "tensor"), scatter_dimension=0, tiled=True
        ),
        lax.psum_scatter(
            partial_value[1], ("dp", "seq", "tensor"), scatter_dimension=0, tiled=True
        ),
    )
    share_len = totals.shape[0]
    offset_rows = lax.axis_index("tensor") * share_len
    seg_share = lax.dynamic_slice_in_dim(seg_row, offset_rows, share_len)
    pos_share = lax.dynamic_slice_in_dim(positions, offset_rows, share_len)
    next_segment = seg_share + 1
    doc_end = jnp.sum(
        jnp.where(slot_ids[None, :] == next_segment[:, None], starts[None, :], 0), axis=1
    )
    doc_end = doc_end + jnp.where(next_segment == seg_count, tok_rows * seq_size, 0)
    counted = (pos_share + 1 < doc_end).astype(jnp.float32)
    logprob = counted * (chosen - jnp.log(totals))
    doc_of = jnp.sum(
        jnp.where(slot_ids[None, :] == seg_share[:, None], doc_index[0][None, :], 0), axis=1
    )
    doc_total = seg_count * lax.axis_size("dp")
    doc_match = (doc_of[:, None] == jnp.arange(doc_total, dtype=jnp.int32)[None, :]).astype(
        jnp.float32
    )
    doc_loglik, doc_counts = lax.psum(
        (
            jnp.sum(logprob[:, None] * doc_match, axis=0),
            jnp.sum(counted[:, None] * doc_match, axis=0),
        ),
        ("dp", "seq", "tensor"),
    )
    token_logprob = lax.all_gather(logprob, "tensor", axis=0, tiled=True)
    return (token_logprob[None, :], doc_loglik, doc_counts)


def solution(mesh):
    in_specs = (
        P(("dp", "seq"), "tensor"),
        P(("dp", "seq"), "tensor"),
        P(("dp", "seq"), "tensor"),
        P(None, "tensor"),
        P(("dp", "seq"), "tensor"),
        P("tensor"),
        P("tensor"),
        P(("dp", "seq", "tensor"), None),
        P("dp", "seq"),
        P("dp", None),
        P("dp", None),
        P(),
    )
    out_specs = (P("dp", "seq"), P(), P())
    return jax.shard_map(local, mesh=mesh, in_specs=in_specs, out_specs=out_specs, check_vma=False)
```

profile of v0, /device:TPU:0, one launch (start us, length us, event | category | flops | bytes accessed | tf_op | source)
XLA Modules:
  0.0 233.8 jit_solution(7810211994765627650)
XLA Ops:
  7.2 0.0 all-gather.2.cloned.1.call-start
  7.2 17.0 %all_gather.18 = bf16[224,1024]{1,0:T(8,128)(2,1)S(1)} all-gather(bf16[56,1024]{1,0:T(8,128)(2,1)} %param.13), channel_id=1, replica_groups=mesh['dp'=4,'seq'=4,'tensor'=2] {'seq'}, dimensions={0}, use_global_device_ids=true | all-gather | bytes 573440 | tf_op jit(solution)/shard_map/all_gather | solution.py:42
  24.2 0.3 reshape.78
  24.6 1.1 reshape.79
  25.7 0.0 copy-start
  25.7 0.0 copy-start.1
  25.7 15.9 %all_gather.19 = bf16[224,1024]{1,0:T(8,128)(2,1)S(1)} all-gather(bf16[56,1024]{1,0:T(8,128)(2,1)} %param.14), channel_id=1, replica_groups=mesh['dp'=4,'seq'=4,'tensor'=2] {'seq'}, dimensions={0}, use_global_device_ids=true | all-gather | bytes 573440 | tf_op jit(solution)/shard_map/all_gather | solution.py:43
  41.6 0.3 reshape.80
  42.0 0.8 select_reduce_fusion.3
  42.7 0.1 fusion.18
  42.8 0.4 fusion.27
  43.2 0.2 fusion.8
  43.5 0.2 copy.27
  43.7 0.2 convert_element_type.22
  43.8 6.7 %all_gather.20 = bf16[56,4096]{1,0:T(8,128)(2,1)S(1)} all-gather(bf16[56,2048]{1,0:T(8,128)(2,1)S(1)} %convert_element_type.22), channel_id=1, replica_groups=mesh['dp'=4,'seq'=4,'tensor'=2] {'tensor'}, dimensions={1}, use_global_device_ids=true | all-gather | bytes 688128 | tf_op jit(solution)/shard_map/all_gather | solution.py:68
  50.5 0.0 copy-done
  50.5 0.0 copy-done.1
  50.5 0.0 copy-start.2
  50.5 0.0 copy-start.3
  50.5 0.0 copy-start.7
  50.5 0.0 copy-start.4
  50.6 0.0 copy-start.5
  50.6 0.0 copy-start.6
  50.6 7.9 %fusion.15 = (f32[56]{0:T(128)S(1)}, f32[56]{0:T(128)S(1)}, f32[56]{0:T(128)S(1)}, f32[56]{0:T(128)S(1)}, f32[56,1792]{1,0:T(8,128)S(1)}) fusion(bf16[56,1792]{1,0:T(8,128)(2,1)S(1)} %copy-done, f32[1792]{0:T(1024)S(1)} %copy-done.1, bf16[56,4096]{1,0:T(8,128)(2,1)S(1)} %all_gather.20, bf16[4096,1792]{1,0:T(8,128)(2,1)} %param.15), kind=kOutput, calls=%fused_computation.23 | convolution fusion | flops 823086848 | bytes 15748992 | tf_op jit(solution)/shard_map/dot_general | solution.py:67
  58.5 4.9 %all-reduce.5 = (f32[56]{0:T(128)S(1)}, f32[56]{0:T(128)S(1)}, f32[56]{0:T(128)S(1)}, f32[56]{0:T(128)S(1)}) all-reduce(f32[56]{0:T(128)S(1)} %get-tuple-element.6, f32[56]{0:T(128)S(1)} %get-tuple-element.8, f32[56]{0:T(128)S(1)} %get-tuple-element.5, f32[56]{0:T(128)S(1)} %get-tuple-element.7), channel_id=1, replica_groups=mesh['dp'=4,'seq'=4,'tensor'=2] {'tensor'}, use_global_device_ids=true, to_apply=%region_10.11 | all-reduce | flops 224 | bytes 1792 | tf_op jit(solution)/shard_map/psum | solution.py:74
  63.5 0.0 copy-done.2
  63.5 0.2 fusion.13
  63.6 6.5 %all_gather.21 = bf16[56,3584]{1,0:T(8,128)(2,1)} all-gather(bf16[56,1792]{1,0:T(8,128)(2,1)S(1)} %fusion.13), channel_id=1, replica_groups=mesh['dp'=4,'seq'=4,'tensor'=2] {'tensor'}, dimensions={1}, use_global_device_ids=true | all-gather | bytes 602112 | tf_op jit(solution)/shard_map/all_gather | solution.py:97
  70.1 0.0 all-gather.2.cloned.1.call-update
  70.2 0.0 copy-done.3
  70.2 0.1 eq.77
  70.2 0.0 copy-done.7
  70.3 0.6 dynamic-slice.1
  71.5 0.0 copy-done.4
  71.5 0.1 broadcast_add_fusion
  71.6 0.0 copy-done.5
  71.6 0.0 copy-done.6
  71.6 0.1 select_reduce_fusion.2
  71.7 0.1 fusion.23
  71.8 62.1 %all-gather.2.cloned.1.call-done = bf16[896,3584]{1,0:T(8,128)(2,1)} async-done(((bf16[56,3584]{1,0:T(8,128)(2,1)}), bf16[896,3584]{1,0:T(8,128)(2,1)}) %all-gather.2.cloned.1.call-update) | async-done | bytes 6422544 | tf_op jit(solution)/shard_map/all_gather | solution.py:98
  133.9 8.1 %fusion = (f32[896]{0:T(1024)S(1)}, f32[896]{0:T(1024)S(1)}) fusion(s32[896]{0:T(1024)S(1)} %eq.77, s32[500]{0:T(512)S(1)} %iota_add_fusion, bf16[896,3584]{1,0:T(8,128)(2,1)} %all-gather.2.cloned.1.call-done, bf16[500,3584]{1,0:T(8,128)(2,1)} %param.19), kind=kOutput, calls=%fused_computation.2 | convolution fusion | flops 3213949952 | bytes 10019280 | tf_op jit(solution)/shard_map/dot_general | solution.py:99
  142.0 39.3 %all-reduce.4 = (f32[896]{0:T(1024)S(1)}, f32[896]{0:T(1024)S(1)}) all-reduce(f32[896]{0:T(1024)S(1)} %get-tuple-element.4, f32[896]{0:T(1024)S(1)} %get-tuple-element.3), channel_id=3, replica_groups=mesh['dp'=4,'seq'=4,'tensor'=2] {'dp','seq','tensor'}, use_global_device_ids=true, to_apply=%region_14.15.clone | all-reduce | flops 1792 | bytes 14336
  181.3 0.2 fusion.25
  181.5 5.7 %all-reduce = f32[56]{0:T(128)} all-reduce(f32[56]{0:T(128)S(1)} %get-tuple-element.21), channel_id=1, replica_groups=mesh['dp'=4,'seq'=4,'tensor'=2] {'tensor'}, use_global_device_ids=true, to_apply=%add | all-reduce | flops 56 | bytes 448
  187.2 0.1 select_reduce_fusion
  187.3 39.7 %all-reduce.3 = (f32[32]{0:T(128)}, f32[32]{0:T(128)}) all-reduce(f32[32]{0:T(128)S(1)} %get-tuple-element.10, f32[32]{0:T(128)S(1)} %get-tuple-element.9), channel_id=1, replica_groups=mesh['dp'=4,'seq'=4,'tensor'=2] {'dp','seq','tensor'}, use_global_device_ids=true, to_apply=%region_17.18 | all-reduce | flops 64 | bytes 512 | tf_op jit(solution)/shard_map/psum | solution.py:132
  (4 shorter events, 0.0 us)
Async XLA Ops:
  7.2 126.7 %all-gather.2.cloned.1.call-start = ((), (), s32[]{:S(2)}) async-start(), calls=%async_computation | async-start | bytes 6823936 | tf_op jit(solution)/shard_map/all_gather | solution.py:98
  25.7 24.8 %copy-start = (bf16[56,1792]{1,0:T(8,128)(2,1)S(1)}, bf16[56,1792]{1,0:T(8,128)(2,1)}, u32[]{:S(2)}) copy-start(bf16[56,1792]{1,0:T(8,128)(2,1)} %param.16) | copy-start | bytes 602116
  25.7 24.8 %copy-start.1 = (f32[1792]{0:T(1024)S(1)}, f32[1792]{0:T(1024)}, u32[]{:S(2)}) copy-start(f32[1792]{0:T(1024)} %param.17) | copy-start | bytes 21508
  50.5 12.9 %copy-start.2 = (f32[1792]{0:T(1024)S(1)}, f32[1792]{0:T(1024)}, u32[]{:S(2)}) copy-start(f32[1792]{0:T(1024)} %param.18) | copy-start | bytes 21508
  50.5 19.6 %copy-start.3 = (s32[4,224]{1,0:T(4,128)S(1)}, s32[4,224]{1,0:T(4,128)}, u32[]{:S(2)}) copy-start(s32[4,224]{1,0:T(4,128)} %param.23) | copy-start | bytes 10756
  50.5 19.7 %copy-start.7 = (u32[32]{0:T(128)S(1)}, u32[32]{0:T(128)}, u32[]{:S(2)}) copy-start(u32[32]{0:T(128)} %constant.64) | copy-start | bytes 388
  50.5 21.0 %copy-start.4 = (s32[1,56]{1,0:T(1,128)S(1)}, s32[1,56]{1,0:T(1,128)}, u32[]{:S(2)}) copy-start(s32[1,56]{1,0:T(1,128)} %param.20) | copy-start | bytes 676
  50.6 21.0 %copy-start.5 = (s32[1,8]{1,0:T(1,128)S(1)}, s32[1,8]{1,0:T(1,128)}, u32[]{:S(2)}) copy-start(s32[1,8]{1,0:T(1,128)} %param.22) | copy-start | bytes 100
  50.6 21.0 %copy-start.6 = (s32[1,8]{1,0:T(1,128)S(1)}, s32[1,8]{1,0:T(1,128)}, u32[]{:S(2)}) copy-start(s32[1,8]{1,0:T(1,128)} %param.21) | copy-start | bytes 100
Sparse Core Ops, SparseCore 0:
  70.3 63.5 all-gather.1
where the time goes:
time: 234 us
  blocking collectives  136 us (58%)
  waiting for transfers between devices  62.1 us (27%)
  matrix products  16.7 us (7%)
  between operations  14.9 us (6%)
  local copies, waits for them, and re-layouts  2.81 us (1%)
    all_gather x1, waiting for transfers between devices, local(): block_in = lax.all_gather(features, ('dp', 'seq'), axis=0, tiled=True)  62.1 us
    unnamed x2, blocking collectives  45 us
    psum x1, blocking collectives, local(): lax.psum((jnp.sum(logprob[:, None] * doc_match, axis=0), jnp.sum(counted[...  39.7 us
    all_gather x1, blocking collectives, local(): key_block = lax.all_gather(key_vectors, 'seq', axis=0, tiled=True)  17 us
    all_gather x1, blocking collectives, local(): value_block = lax.all_gather(value_vectors, 'seq', axis=0, tiled=True)  15.9 us
    dot_general x1, matrix products, local(): lax.dot_general(vocab_weight, block_in, (((1,), (1,)), ((), ())), preferr...  8.11 us
    dot_general x1, matrix products, local(): jnp.dot(lax.all_gather(attended, 'tensor', axis=1, tiled=True), out_weigh...  7.92 us
    all_gather x1, blocking collectives, local(): lax.all_gather(attended, 'tensor', axis=1, tiled=True)  6.69 us
  transfers between devices with their start and end apart: 1, of which 1 were waited for; matrix products, arithmetic and copies ran while one was open for 0% of the time, Pallas kernels for 0%

commit v1 on v0

v1 whole, which is shorter than its diff:
```python
import functools

import jax
import jax.numpy as jnp
from jax import lax
from jax.experimental import pallas as pl
from jax.experimental.pallas import tpu as pltpu
from jax.sharding import PartitionSpec as P

HEAD_DIM = 256
ATTENTION_CAP = 50.0
LOGIT_CAP = 30.0
EPSILON = 1e-06
MESH = pl.DeviceIdType.MESH
PAD = 64
NT = (((1,), (1,)), ((), ()))
NN = (((1,), (0,)), ((), ()))


def dot(a, b, dims):
    return lax.dot_general(a, b, dims, preferred_element_type=jnp.float32)


def body(
    sizes,
    q_ref, k_ref, v_ref, w_hbm, res_ref, pg_ref, fg_ref, voc_hbm, first_ref, lab_ref, meta_ref,
    lp_ref, docs_ref,
    w_ref, voc_ref, kv, num, den, att, branch, stat, hid, part, gat_dp, gat_t, gat_s,
    local_sem, kv_send, kv_recv, att_send, att_recv, st_send, st_recv,
    hid_recv, z_send, y_send, x_send, c_send,
    fd_send, fd_recv, ft_send, ft_recv, fs_send, fs_recv,
):
    ND, NZ, NY, docs = sizes
    NC = 2 if ND % 2 == 0 else 1
    NX = ND // NC
    D = voc_hbm.shape[-1] if voc_hbm.ndim == 2 else voc_hbm.shape[0] * voc_hbm.shape[2]
    me_d, me_z, me_t = lax.axis_index("dp"), lax.axis_index("seq"), lax.axis_index("tensor")
    me_x, me_c = me_d // NC, me_d % NC
    rows = q_ref.shape[0]
    kvw = k_ref.shape[1]
    groups = kvw // HEAD_DIM
    per = q_ref.shape[1] // kvw
    heads = groups * per
    qw = q_ref.shape[1]
    fw = w_hbm.shape[1]

    w_copy = pltpu.make_async_copy(w_hbm, w_ref, local_sem.at[0])
    voc_copy = pltpu.make_async_copy(voc_hbm, voc_ref, local_sem.at[1])
    w_copy.start()
    voc_copy.start()

    def dev(d=None, z=None, t=None):
        return (me_d if d is None else d, me_z if z is None else z, me_t if t is None else t)

    def remote(src, dst, send, recv, device):
        return pltpu.make_async_remote_copy(
            src_ref=src, dst_ref=dst, send_sem=send, recv_sem=recv, device_id=device, device_id_type=MESH
        )

    def others(me, n):
        return [lax.rem(me + i, n) for i in range(1, n)]

    barrier = pltpu.get_barrier_semaphore()
    peers = [dev(d=p) for p in others(me_d, ND)]
    peers += [dev(z=p) for p in others(me_z, NZ)]
    peers += [dev(t=p) for p in others(me_t, NY)]
    for p in peers:
        pl.semaphore_signal(barrier, inc=1, device_id=p, device_id_type=MESH)
    pl.semaphore_wait(barrier, len(peers))

    def kv_copy(s, which):
        src = (k_ref, v_ref)[which] if s == 0 else kv.at[s, which]
        return remote(
            src, kv.at[s + 1, which], kv_send.at[s, which], kv_recv.at[s + 1, which],
            dev(z=lax.rem(me_z + 1, NZ)),
        )

    i_pos = lax.broadcasted_iota(jnp.int32, (rows, rows), 0)
    j_pos = lax.broadcasted_iota(jnp.int32, (rows, rows), 1)
    first = first_ref[...]
    for s in range(NZ):
        @pl.when(me_z >= s)
        def _(s=s):
            for which in range(2):
                if s > 0:
                    remote(
                        kv.at[s, which], kv.at[s, which], kv_send.at[s - 1, which], kv_recv.at[s, which], dev()
                    ).wait_recv()
                if s < NZ - 1:
                    @pl.when(me_z + 1 < NZ)
                    def _():
                        kv_copy(s, which).start()
            key_pos = (me_z - s) * rows + j_pos
            seen = key_pos >= first
            if s == 0:
                seen = seen & (j_pos <= i_pos)
            for h in range(heads):
                cols = slice(h // per * HEAD_DIM, (h // per + 1) * HEAD_DIM)
                kk = k_ref[:, cols] if s == 0 else kv[s, 0, :, cols]
                vv = v_ref[:, cols] if s == 0 else kv[s, 1, :, cols]
                raw = dot(q_ref[:, h * HEAD_DIM:(h + 1) * HEAD_DIM], kk, NT)
                capped = ATTENTION_CAP * jnp.tanh(raw * (HEAD_DIM ** (-0.5) / ATTENTION_CAP))
                wt = jnp.where(seen, jnp.exp(capped), 0.0)
                top = dot(wt.astype(jnp.bfloat16), vv, NN)
                low = jnp.broadcast_to(jnp.sum(wt, axis=1, keepdims=True), (rows, 128))
                if s == 0:
                    num[h] = top
                    den[h] = low
                else:
                    num[h] = num[h] + top
                    den[h] = den[h] + low

    def att_copy(part_id, peer, idx):
        width = qw // 2
        ref = att.at[me_t, :, pl.ds(part_id * width, width)]
        return remote(ref, ref, att_send.at[idx, part_id], att_recv.at[me_t, part_id], dev(t=peer))

    for half in range(2):
        for h in range(half * heads // 2, (half + 1) * heads // 2):
            att[me_t, :, h * HEAD_DIM:(h + 1) * HEAD_DIM] = (num[h] / den[h][:, :1]).astype(jnp.bfloat16)
        for i, p in enumerate(others(me_t, NY)):
            att_copy(half, p, i).start()

    w_copy.wait()
    step = 256 if fw % 256 == 0 else fw

    def project(t, begin):
        base = pl.multiple_of(t * qw, qw)
        for n in range(fw // step):
            got = dot(att[t], w_ref[pl.ds(base, qw), n * step:(n + 1) * step], NN)
            cols = slice(n * step, (n + 1) * step)
            branch[:, cols] = got if begin else branch[:, cols] + got

    project(me_t, True)
    for p in others(me_t, NY):
        for half in range(2):
            width = qw // 2
            ref = att.at[p, :, pl.ds(half * width, width)]
            remote(ref, ref, att_send.at[0, 0], att_recv.at[p, half], dev()).wait_recv()
        project(p, False)

    br = branch[...]
    carried = res_ref[...].astype(jnp.float32)
    gained = pg_ref[...] * br
    lane = lax.broadcasted_iota(jnp.int32, (rows, 128), 1)
    packed = jnp.zeros((rows, 128), jnp.float32)
    for i, prod in enumerate((br * br, carried * carried, carried * gained, gained * gained)):
        packed = jnp.where(lane == i, jnp.sum(prod, axis=1, keepdims=True), packed)
    stat[me_t] = packed

    def stat_copy(peer, i):
        return remote(stat.at[me_t], stat.at[me_t], st_send.at[i], st_recv.at[me_t], dev(t=peer))

    for i, p in enumerate(others(me_t, NY)):
        stat_copy(p, i).start()
    for p in others(me_t, NY):
        remote(stat.at[p], stat.at[p], st_send.at[0], st_recv.at[p], dev()).wait_recv()
    total = stat[0]
    for t in range(1, NY):
        total = total + stat[t]
    sq_branch, sq_carried, cross, sq_gained = (total[:, i:i + 1] for i in range(4))
    inv_branch = 1.0 / jnp.sqrt(sq_branch / D + EPSILON)
    sq_total = sq_carried + 2.0 * inv_branch * cross + inv_branch * inv_branch * sq_gained
    inv_total = 1.0 / jnp.sqrt(sq_total / D + EPSILON)
    hid[me_d, me_z, me_t, :rows, :] = (
        fg_ref[...] * (carried + gained * inv_branch) * inv_total
    ).astype(jnp.bfloat16)

    def slot(d, z, t):
        return hid.at[d, z, t, pl.ds(0, rows), :]

    def send(d, z, t, sem, device):
        return remote(slot(d, z, t), slot(d, z, t), sem, hid_recv.at[d, z, t], device)

    def landed(d, z, t):
        send(d, z, t, z_send.at[0, 0], dev()).wait_recv()

    y_peers = others(me_t, NY)
    x_peers = [p * NC + me_c for p in others(me_x, NX)]
    twin = [me_x * NC + 1 - me_c] if NC == 2 else []
    offsets = [0]
    for i in range(1, NZ):
        offsets += [-i, i]

    def y_first(z):
        return lax.rem(z + me_c, 2) == 0

    def guarded(off, fn):
        if off == 0:
            fn(me_z)
        else:
            @pl.when((me_z + off >= 0) & (me_z + off < NZ))
            def _():
                fn(me_z + off)

    def to_twin(d, z, t, act):
        for p in twin:
            act(send(d, z, t, c_send.at[d // NC, z, t], dev(d=p)))

    def column(z, off, act, wait):
        if wait and off != 0:
            landed(me_d, z, me_t)
        if off <= 0:
            @pl.when(me_z + 1 < NZ)
            def _():
                act(send(me_d, z, me_t, z_send.at[z, 0], dev(z=lax.rem(me_z + 1, NZ))))
        if off >= 0:
            @pl.when(me_z >= 1)
            def _():
                act(send(me_d, z, me_t, z_send.at[z, 1], dev(z=lax.rem(me_z + NZ - 1, NZ))))
        for i, p in enumerate(y_peers):
            act(send(me_d, z, me_t, y_send.at[0, z, i], dev(t=p)))
        for i, p in enumerate(x_peers):
            act(send(me_d, z, me_t, x_send.at[0, z, i], dev(d=p)))
        to_twin(me_d, z, me_t, act)

    def across(z, act, wait):
        for j, t in enumerate(y_peers):
            if wait:
                landed(me_d, z, t)
            if x_peers:
                @pl.when(y_first(z))
                def _(j=j, t=t):
                    for i, p in enumerate(x_peers):
                        act(send(me_d, z, t, x_send.at[1 + j, z, i], dev(d=p)))
            to_twin(me_d, z, t, act)
        for j, d in enumerate(x_peers):
            if wait:
                landed(d, z, me_t)
            if y_peers:
                @pl.when(jnp.logical_not(y_first(z)))
                def _(j=j, d=d):
                    for i, p in enumerate(y_peers):
                        act(send(d, z, me_t, y_send.at[1 + j, z, i], dev(t=p)))
            to_twin(d, z, me_t, act)

    def diagonal(z, act, wait):
        for d in x_peers:
            for t in y_peers:
                if wait:
                    landed(d, z, t)
                to_twin(d, z, t, act)

    def start(c):
        c.start()

    guarded(offsets[0], lambda z: column(z, 0, start, True))
    for n in range(1, len(offsets) + 1):
        if n < len(offsets):
            guarded(offsets[n], lambda z: column(z, offsets[n], start, True))
        guarded(offsets[n - 1], lambda z: across(z, start, True))

    voc_copy.wait()
    count = voc_ref.shape[-2]
    base = ((me_d * NZ + me_z) * NY + me_t) * count
    vocab_ids = base + lax.broadcasted_iota(jnp.int32, (count, NZ * PAD), 0)
    per_row = NZ * PAD // 128
    R = ND * per_row

    def logits_of(d):
        acc = None
        for t in range(NY):
            left = voc_ref[:, t * fw:(t + 1) * fw] if len(voc_ref.shape) == 2 else voc_ref[t]
            got = dot(left, hid[d, :, t].reshape(NZ * PAD, fw), NT)
            acc = got if acc is None else acc + got
        capped = LOGIT_CAP * jnp.tanh(acc * (1.0 / LOGIT_CAP))
        tot = jnp.sum(jnp.exp(capped), axis=0, keepdims=True)
        cho = jnp.sum(jnp.where(vocab_ids == lab_ref[d], capped, 0.0), axis=0, keepdims=True)
        for r in range(per_row):
            part[pl.ds(d * per_row + r, 1), :] = tot[:, r * 128:(r + 1) * 128]
            part[pl.ds(R + d * per_row + r, 1), :] = cho[:, r * 128:(r + 1) * 128]

    logits_of(me_d)
    for d in twin:
        for z in range(NZ):
            for t in range(NY):
                landed(d, z, t)
        logits_of(d)
    for off in offsets:
        guarded(off, lambda z: diagonal(z, start, True))
    for d in x_peers:
        logits_of(d)
    if NC == 2:
        for p in others(me_x, NX):
            d = p * NC + 1 - me_c
            for z in range(NZ):
                for t in range(NY):
                    landed(d, z, t)
            logits_of(d)
    part[2 * R:4 * R, :] = meta_ref[...]

    def exchange(buf, me, n, sends, recvs, where):
        buf[me] = part[...]

        def copy(p, i):
            return remote(buf.at[me], buf.at[me], sends.at[i], recvs.at[me], where(p))

        for i, p in enumerate(others(me, n)):
            copy(p, i).start()
        for p in others(me, n):
            remote(buf.at[p], buf.at[p], sends.at[0], recvs.at[p], dev()).wait_recv()
        out = buf[0]
        for j in range(1, n):
            out = out + buf[j]
        part[...] = out
        return lambda: [copy(p, i).wait_send() for i, p in enumerate(others(me, n))]

    drains = [
        exchange(gat_dp, me_d, ND, fd_send, fd_recv, lambda p: dev(d=p)),
        exchange(gat_t, me_t, NY, ft_send, ft_recv, lambda p: dev(t=p)),
        exchange(gat_s, me_z, NZ, fs_send, fs_recv, lambda p: dev(z=p)),
    ]
    totals, chosen = part[0:R, :], part[R:2 * R, :]
    counted, doc = part[2 * R:3 * R, :], part[3 * R:4 * R, :]
    inside = lax.rem(lax.broadcasted_iota(jnp.int32, (R, 128), 1), PAD) < rows
    counted = jnp.where(inside, counted, 0.0)
    logprob = jnp.where(inside, counted * (chosen - jnp.log(totals)), 0.0)
    lp_ref[...] = logprob
    names = lax.broadcasted_iota(jnp.int32, (docs, 128), 0).astype(jnp.float32)
    like = jnp.zeros((docs, 128), jnp.float32)
    cnt = jnp.zeros((docs, 128), jnp.float32)
    for r in range(R):
        hit = names == doc[r:r + 1, :]
        like = like + jnp.where(hit, logprob[r:r + 1, :], 0.0)
        cnt = cnt + jnp.where(hit, counted[r:r + 1, :], 0.0)
    col = lax.broadcasted_iota(jnp.int32, (docs, 128), 1)
    docs_ref[...] = jnp.where(
        col == 0, jnp.sum(like, axis=1, keepdims=True), jnp.sum(cnt, axis=1, keepdims=True)
    )

    def drain(c):
        c.wait_send()

    for s in range(NZ - 1):
        @pl.when((me_z >= s) & (me_z + 1 < NZ))
        def _(s=s):
            for which in range(2):
                kv_copy(s, which).wait_send()
    for i, p in enumerate(others(me_t, NY)):
        for half in range(2):
            att_copy(half, p, i).wait_send()
        stat_copy(p, i).wait_send()
    for off in offsets:
        guarded(off, lambda z: column(z, off, drain, False))
        guarded(off, lambda z: across(z, drain, False))
        guarded(off, lambda z: diagonal(z, drain, False))
    for d in drains:
        d()


def local(
    mesh, query_vectors, key_vectors, value_vectors, out_weight, residual, post_gain, final_gain,
    vocab_weight, segment_ids, doc_starts, doc_index, targets,
):
    ND, NZ, NY = mesh.shape["dp"], mesh.shape["seq"], mesh.shape["tensor"]
    rows = query_vectors.shape[0]
    seg_row, starts = segment_ids[0], doc_starts[0]
    seg_count = starts.shape[0]
    docs = seg_count * ND
    slots = jnp.arange(seg_count, dtype=jnp.int32)
    me_d, me_z, me_t = lax.axis_index("dp"), lax.axis_index("seq"), lax.axis_index("tensor")
    positions = me_z * rows + jnp.arange(rows, dtype=jnp.int32)
    match = seg_row[:, None] == slots[None, :]
    doc_first = jnp.sum(jnp.where(match, starts[None, :], 0), axis=1, keepdims=True)
    ends = jnp.concatenate([starts[1:], jnp.full((1,), rows * NZ, jnp.int32)])
    doc_end = jnp.sum(jnp.where(match, ends[None, :], 0), axis=1)
    counted = (positions + 1 < doc_end).astype(jnp.float32)
    doc_of = jnp.sum(jnp.where(match, doc_index[0][None, :], 0), axis=1).astype(jnp.float32)
    blocks = ND * NZ
    mine = (jnp.arange(blocks)[None, :, None] == me_d * NZ + me_z) & (me_t == 0)
    facts = jnp.pad(jnp.stack([counted, doc_of]), ((0, 0), (0, PAD - rows)))
    meta = jnp.where(mine, facts[:, None, :], 0.0).reshape(2 * blocks * PAD // 128, 128)
    labels = jnp.pad(targets.reshape(ND, NZ, rows), ((0, 0), (0, 0), (0, PAD - rows))).reshape(ND, 1, NZ * PAD)
    fw = out_weight.shape[1]
    voc = vocab_weight
    if fw % 128 != 0:
        voc = voc.reshape(voc.shape[0], NY, fw).transpose(1, 0, 2)
    kvw, qw = key_vectors.shape[1], query_vectors.shape[1]
    heads = qw // HEAD_DIM
    NC = 2 if ND % 2 == 0 else 1
    NX = ND // NC
    R = blocks * PAD // 128
    f32, bf16 = jnp.float32, jnp.bfloat16
    dma = pltpu.SemaphoreType.DMA
    vm = pl.BlockSpec(memory_space=pltpu.VMEM)
    anyspace = pl.BlockSpec(memory_space=pl.ANY)
    logprob, sums = pl.pallas_call(
        functools.partial(body, (ND, NZ, NY, docs)),
        out_shape=(jax.ShapeDtypeStruct((R, 128), f32), jax.ShapeDtypeStruct((docs, 128), f32)),
        in_specs=[vm, vm, vm, anyspace, vm, vm, vm, anyspace, vm, vm, vm],
        out_specs=(vm, vm),
        scratch_shapes=[
            pltpu.VMEM(out_weight.shape, bf16),
            pltpu.VMEM(voc.shape, bf16),
            pltpu.VMEM((NZ, 2, rows, kvw), bf16),
            pltpu.VMEM((heads, rows, HEAD_DIM), f32),
            pltpu.VMEM((heads, rows, 128), f32),
            pltpu.VMEM((NY, rows, qw), bf16),
            pltpu.VMEM((rows, fw), f32),
            pltpu.VMEM((NY, rows, 128), f32),
            pltpu.VMEM((ND, NZ, NY, PAD, fw), bf16),
            pltpu.VMEM((4 * R, 128), f32),
            pltpu.VMEM((ND, 4 * R, 128), f32),
            pltpu.VMEM((NY, 4 * R, 128), f32),
            pltpu.VMEM((NZ, 4 * R, 128), f32),
            dma((2,)),
            dma((NZ, 2)), dma((NZ, 2)),
            dma((NY, 2)), dma((NY, 2)),
            dma((NY,)), dma((NY,)),
            dma((ND, NZ, NY)),
            dma((NZ, 2)),
            dma((NX, NZ, NY)),
            dma((NY, NZ, NX)),
            dma((NX, NZ, NY)),
            dma((ND,)), dma((ND,)),
            dma((NY,)), dma((NY,)),
            dma((NZ,)), dma((NZ,)),
        ],
        compiler_params=pltpu.CompilerParams(
            collective_id=0, has_side_effects=True, vmem_limit_bytes=60 * 1024 * 1024
        ),
        name="packed_loglik",
    )(
        query_vectors, key_vectors, value_vectors, out_weight, residual, post_gain[None, :],
        final_gain[None, :], voc, doc_first, labels, meta,
    )
    mine_lp = lax.dynamic_slice_in_dim(logprob.reshape(blocks, PAD), me_d * NZ + me_z, 1, axis=0)
    return (mine_lp[:, :rows], sums[:, 0], sums[:, 1])


def solution(mesh):
    in_specs = (
        P(("dp", "seq"), "tensor"),
        P(("dp", "seq"), "tensor"),
        P(("dp", "seq"), "tensor"),
        P(None, "tensor"),
        P(("dp", "seq"), "tensor"),
        P("tensor"),
        P("tensor"),
        P(("dp", "seq", "tensor"), None),
        P("dp", "seq"),
        P("dp", None),
        P("dp", None),
        P(),
    )
    out_specs = (P("dp", "seq"), P(), P())
    return jax.shard_map(
        functools.partial(local, mesh), mesh=mesh, in_specs=in_specs, out_specs=out_specs, check_vma=False
    )
```

time: 234 us -> 89.2 us (0.38)
  blocking collectives: 136 us -> 0 us
  Pallas kernels: 0 us -> 78.1 us
  waiting for transfers between devices: 62.1 us -> 0 us
  matrix products: 16.7 us -> 0 us
  between operations: 14.9 us -> 0.68 us
  local copies, waits for them, and re-layouts: 2.81 us -> 8.89 us
    pallas_call x0 -> x1, Pallas kernels: none -> 78.1 us  [local(): pl.pallas_call(functools.partial(body, (ND, NZ, NY, docs)), out_shape=(ja...]
    all_gather x1 -> x0, waiting for transfers between devices: 62.1 us -> none  [local(): block_in = lax.all_gather(features, ('dp', 'seq'), axis=0, tiled=True)]
    all_gather x4 -> x0, blocking collectives: 46.1 us -> none  [the longest x1 17 us: local(): key_block = lax.all_gather(key_vectors, 'seq', axis=0, tiled=True)]
    unnamed x2 -> x0, blocking collectives: 45 us -> none
    psum x2 -> x0, blocking collectives: 44.6 us -> none  [the longest x1 39.7 us: local(): lax.psum((jnp.sum(logprob[:, None] * doc_match, axis=0), jnp.sum(counted[...]
    dot_general x4 -> x0, matrix products: 16.7 us -> none  [the longest x1 8.11 us: local(): lax.dot_general(vocab_weight, block_in, (((1,), (1,)), ((), ())), preferr...]
    broadcast_in_dim x0 -> x3, local copies, waits for them, and re-layouts: none -> 3.28 us  [the longest x1 1.29 us: local(): post_gain[None, :]]
  transfers between devices with their start and end apart: 1 -> 0, of which waited for: 1 -> 0; matrix products, arithmetic and copies ran while one was open for 0% -> 0% of each run, Pallas kernels for 0% -> 0%
where the time goes in v1:
time: 89.2 us; the launch traced here: 88.7 us
  Pallas kernels  78.1 us (88%)
  local copies, waits for them, and re-layouts  8.89 us (10%)
  other arithmetic  0.95 us (1%)
    pallas_call x1, Pallas kernels, local(): pl.pallas_call(functools.partial(body, (ND, NZ, NY, docs)), out_shape=(ja...  78.1 us

profile of v1, /device:TPU:0, one launch (start us, length us, event | category | flops | bytes accessed | tf_op | source)
XLA Modules:
  0.0 88.7 jit_solution(15421514416036159651)
XLA Ops:
  0.7 0.7 slice_bitcast_fusion
  1.4 0.1 pad_add_fusion
  1.5 0.8 select_reduce_fusion.1
  2.3 1.3 %broadcast_in_dim.61.pg_ref = f32[1,1792]{1,0:T(1,128)} reshape(f32[1792]{0:T(1024)} %param.17) | data formatting | bytes 14336 | tf_op jit(solution)/shard_map/broadcast_in_dim | solution.py:424
  3.6 1.3 %broadcast_in_dim.62.fg_ref = f32[1,1792]{1,0:T(1,128)} reshape(f32[1792]{0:T(1024)} %param.18) | data formatting | bytes 14336 | tf_op jit(solution)/shard_map/broadcast_in_dim | solution.py:425
  4.9 0.8 reshape.59
  5.6 0.7 reshape.60.lab_ref
  6.3 0.1 broadcast_select_fusion
  6.4 0.7 select_n.25.meta_ref
  7.1 0.7 copy.17.first_ref
  7.8 78.1 %packed_loglik.1 = (f32[8,128]{1,0:T(8,128)}, f32[32,128]{1,0:T(8,128)}) custom-call(bf16[56,2048]{1,0:T(8,128)(2,1)} %q_ref.1, bf16[56,1024]{1,0:T(8,128)(2,1)} %k_ref.1, bf16[56,1024]{1,0:T(8,128)(2,1)} %v_ref.1, bf16[4096,1792]{1,0:T(8,128)(2,1)} %w_hbm.1, bf16[56,1792]{1,0:T(8,128)(2,1)} %res_ref.1, f32[1,1792]{1,0:T(1,128)} %broadcast_in_dim.61.pg_ref, ...), custom_call_target="tpu_custom_call" | custom-call | tf_op jit(solution)/shard_map/packed_loglik/pallas_call | solution.py:387
  85.9 1.5 %slice_reduce_fusion = (f32[32]{0:T(128)}, f32[32]{0:T(128)}) fusion(f32[32,128]{1,0:T(8,128)} %get-tuple-element.6), kind=kLoop, calls=%fused_computation | loop fusion | bytes 512 | tf_op jit(solution)/shard_map/slice | solution.py:428
  87.4 0.8 reshape.61
  88.1 0.5 constant_dynamic-slice_fusion
  (5 shorter events, 0.0 us)

commit v2 on v1

--- a/solution.py
+++ b/solution.py
@@ -23,9 +23,9 @@
 
 def body(
     sizes,
-    q_ref, k_ref, v_ref, w_hbm, res_ref, pg_ref, fg_ref, voc_hbm, first_ref, lab_ref, meta_ref,
-    lp_ref, docs_ref,
-    w_ref, voc_ref, kv, num, den, att, branch, stat, hid, part, gat_dp, gat_t, gat_s,
+    q_ref, k_ref, v_ref, w_hbm, res_ref, pg_ref, fg_ref, voc_hbm, seg_ref, start_ref, index_ref, target_ref,
+    lp_ref, like_ref, cnt_ref,
+    w_ref, voc_ref, kv, num, den, att, branch, stat, hid, held, lab_ref, part, gat_dp, gat_t, gat_s,
     local_sem, kv_send, kv_recv, att_send, att_recv, st_send, st_recv,
     hid_recv, z_send, y_send, x_send, c_send,
     fd_send, fd_recv, ft_send, ft_recv, fs_send, fs_recv,
@@ -68,80 +68,136 @@
         pl.semaphore_signal(barrier, inc=1, device_id=p, device_id_type=MESH)
     pl.semaphore_wait(barrier, len(peers))
 
-    def kv_copy(s, which):
-        src = (k_ref, v_ref)[which] if s == 0 else kv.at[s, which]
-        return remote(
-            src, kv.at[s + 1, which], kv_send.at[s, which], kv_recv.at[s + 1, which],
-            dev(z=lax.rem(me_z + 1, NZ)),
-        )
-
+    def kv_copy(block, g):
+        cols = pl.ds(g * HEAD_DIM, HEAD_DIM)
+        up = dev(z=lax.rem(me_z + 1, NZ))
+        if block is None:
+            pairs = [(k_ref.at[:, cols], kv.at[me_z, 0, :, cols]), (v_ref.at[:, cols], kv.at[me_z, 1, :, cols])]
+            where = me_z
+        else:
+            pairs = [(kv.at[block, i, :, cols],) * 2 for i in range(2)]
+            where = block
+        return [
+            remote(src, dst, kv_send.at[where, g, i], kv_recv.at[where, g, i], up)
+            for i, (src, dst) in enumerate(pairs)
+        ]
+
+    @pl.when(me_z + 1 < NZ)
+    def _():
+        for g in range(groups):
+            for c in kv_copy(None, g):
+                c.start()
+
+    seg = seg_ref[...]
+    first_row = jnp.zeros((1, rows), jnp.int32)
+    end_row = jnp.zeros((1, rows), jnp.int32)
+    doc_row = jnp.zeros((1, rows), jnp.int32)
+    segs = start_ref.shape[1]
+    for n in range(segs):
+        here = seg == n
+        first_row = jnp.where(here, start_ref[0, n], first_row)
+        end_row = jnp.where(here, start_ref[0, n + 1] if n + 1 < segs else rows * NZ, end_row)
+        doc_row = jnp.where(here, index_ref[0, n], doc_row)
+    spot = me_z * rows + lax.broadcasted_iota(jnp.int32, (1, rows), 1)
+    code_row = doc_row + jnp.where(spot + 1 < end_row, docs, 0)
     i_pos = lax.broadcasted_iota(jnp.int32, (rows, rows), 0)
     j_pos = lax.broadcasted_iota(jnp.int32, (rows, rows), 1)
-    first = first_ref[...]
-    for s in range(NZ):
-        @pl.when(me_z >= s)
-        def _(s=s):
-            for which in range(2):
-                if s > 0:
-                    remote(
-                        kv.at[s, which], kv.at[s, which], kv_send.at[s - 1, which], kv_recv.at[s, which], dev()
-                    ).wait_recv()
-                if s < NZ - 1:
-                    @pl.when(me_z + 1 < NZ)
-                    def _():
-                        kv_copy(s, which).start()
-            key_pos = (me_z - s) * rows + j_pos
-            seen = key_pos >= first
-            if s == 0:
-                seen = seen & (j_pos <= i_pos)
-            for h in range(heads):
-                cols = slice(h // per * HEAD_DIM, (h // per + 1) * HEAD_DIM)
-                kk = k_ref[:, cols] if s == 0 else kv[s, 0, :, cols]
-                vv = v_ref[:, cols] if s == 0 else kv[s, 1, :, cols]
-                raw = dot(q_ref[:, h * HEAD_DIM:(h + 1) * HEAD_DIM], kk, NT)
-                capped = ATTENTION_CAP * jnp.tanh(raw * (HEAD_DIM ** (-0.5) / ATTENTION_CAP))
-                wt = jnp.where(seen, jnp.exp(capped), 0.0)
-                top = dot(wt.astype(jnp.bfloat16), vv, NN)
-                low = jnp.broadcast_to(jnp.sum(wt, axis=1, keepdims=True), (rows, 128))
-                if s == 0:
-                    num[h] = top
-                    den[h] = low
-                else:
-                    num[h] = num[h] + top
-                    den[h] = den[h] + low
-
-    def att_copy(part_id, peer, idx):
-        width = qw // 2
-        ref = att.at[me_t, :, pl.ds(part_id * width, width)]
-        return remote(ref, ref, att_send.at[idx, part_id], att_recv.at[me_t, part_id], dev(t=peer))
-
-    for half in range(2):
-        for h in range(half * heads // 2, (half + 1) * heads // 2):
+
+    def column_of(row):
+        full = jnp.broadcast_to(row.astype(jnp.float32), (rows, rows))
+        return jnp.sum(jnp.where(i_pos == j_pos, full, 0.0), axis=1, keepdims=True)
+
+    first = column_of(first_row).astype(jnp.int32)
+    per_line = 128 // PAD
+    my_block = me_d * NZ + me_z
+    lanes = lax.broadcasted_iota(jnp.int32, (rows, 128), 1)
+    sub = lax.broadcasted_iota(jnp.int32, (rows, 128), 0)
+    placed = jnp.where(lanes == sub + lax.rem(my_block, per_line) * PAD, column_of(code_row), 0.0)
+    code_line = jnp.sum(placed, axis=0, keepdims=True) * jnp.where(me_t == 0, 1.0, 0.0)
+    gap = jnp.zeros((1, PAD - rows), jnp.int32)
+    for d in range(ND):
+        pieces = []
+        for z in range(NZ):
+            pieces += [target_ref[d:d + 1, z * rows:(z + 1) * rows], gap]
+        lab_ref[d] = jnp.concatenate(pieces, axis=1)
+
+    def attend(block, g):
+        cols = slice(g * HEAD_DIM, (g + 1) * HEAD_DIM)
+        if block is None:
+            kk, vv = k_ref[:, cols], v_ref[:, cols]
+            seen = (me_z * rows + j_pos >= first) & (j_pos <= i_pos)
+        else:
+            kk, vv = kv[block, 0, :, cols], kv[block, 1, :, cols]
+            seen = block * rows + j_pos >= first
+        for h in range(g * per, (g + 1) * per):
+            raw = dot(q_ref[:, h * HEAD_DIM:(h + 1) * HEAD_DIM], kk, NT)
+            capped = ATTENTION_CAP * jnp.tanh(raw * (HEAD_DIM ** (-0.5) / ATTENTION_CAP))
+            wt = jnp.where(seen, jnp.exp(capped), 0.0)
+            top = dot(wt.astype(jnp.bfloat16), vv, NN)
+            low = jnp.broadcast_to(jnp.sum(wt, axis=1, keepdims=True), (rows, 128))
+            if block is None:
+                num[h] = top
+                den[h] = low
+            else:
+                num[h] = num[h] + top
+                den[h] = den[h] + low
+
+    def arrived(block, g):
+        for c in kv_copy(block, g):
+            c.wait_recv()
+
+        @pl.when(me_z + 1 < NZ)
+        def _():
+            for c in kv_copy(block, g):
+                c.start()
+
+    for g in range(groups):
+        attend(None, g)
+    for block in range(NZ - 2, 0, -1):
+        @pl.when(block < me_z)
+        def _(block=block):
+            for g in range(groups):
+                arrived(block, g)
+                attend(block, g)
+
+    gw = per * HEAD_DIM
+
+    def att_copy(g, peer, idx):
+        ref = att.at[me_t, :, pl.ds(g * gw, gw)]
+        return remote(ref, ref, att_send.at[idx, g], att_recv.at[me_t, g], dev(t=peer))
+
+    step = 256 if fw % 256 == 0 else fw
+
+    def project(t, g, begin):
+        base = pl.multiple_of(t * qw + g * gw, gw)
+        left = att[t, :, g * gw:(g + 1) * gw]
+        for n in range(fw // step):
+            cols = slice(n * step, (n + 1) * step)
+            got = dot(left, w_ref[pl.ds(base, gw), cols], NN)
+            branch[:, cols] = got if begin else branch[:, cols] + got
+
+    for g in range(groups):
+        if NZ > 1:
+            @pl.when(me_z > 0)
+            def _(g=g):
+                arrived(0, g)
+                attend(0, g)
+        for h in range(g * per, (g + 1) * per):
             att[me_t, :, h * HEAD_DIM:(h + 1) * HEAD_DIM] = (num[h] / den[h][:, :1]).astype(jnp.bfloat16)
         for i, p in enumerate(others(me_t, NY)):
-            att_copy(half, p, i).start()
-
-    w_copy.wait()
-    step = 256 if fw % 256 == 0 else fw
-
-    def project(t, begin):
-        base = pl.multiple_of(t * qw, qw)
-        for n in range(fw // step):
-            got = dot(att[t], w_ref[pl.ds(base, qw), n * step:(n + 1) * step], NN)
-            cols = slice(n * step, (n + 1) * step)
-            branch[:, cols] = got if begin else branch[:, cols] + got
-
-    project(me_t, True)
-    for p in others(me_t, NY):
-        for half in range(2):
-            width = qw // 2
-            ref = att.at[p, :, pl.ds(half * width, width)]
-            remote(ref, ref, att_send.at[0, 0], att_recv.at[p, half], dev()).wait_recv()
-        project(p, False)
+            att_copy(g, p, i).start()
+        if g == 0:
+            w_copy.wait()
+        project(me_t, g, g == 0)
+    for g in range(groups):
+        for p in others(me_t, NY):
+            ref = att.at[p, :, pl.ds(g * gw, gw)]
+            remote(ref, ref, att_send.at[0, 0], att_recv.at[p, g], dev()).wait_recv()
+            project(p, g, False)
 
     br = branch[...]
     carried = res_ref[...].astype(jnp.float32)
-    gained = pg_ref[...] * br
+    gained = pg_ref[...].reshape(1, fw) * br
     lane = lax.broadcasted_iota(jnp.int32, (rows, 128), 1)
     packed = jnp.zeros((rows, 128), jnp.float32)
     for i, prod in enumerate((br * br, carried * carried, carried * gained, gained * gained)):
@@ -163,7 +219,7 @@
     sq_total = sq_carried + 2.0 * inv_branch * cross + inv_branch * inv_branch * sq_gained
     inv_total = 1.0 / jnp.sqrt(sq_total / D + EPSILON)
     hid[me_d, me_z, me_t, :rows, :] = (
-        fg_ref[...] * (carried + gained * inv_branch) * inv_total
+        fg_ref[...].reshape(1, fw) * (carried + gained * inv_branch) * inv_total
     ).astype(jnp.bfloat16)
 
     def slot(d, z, t):
@@ -257,12 +313,15 @@
     per_row = NZ * PAD // 128
     R = ND * per_row
 
-    def logits_of(d):
-        acc = None
-        for t in range(NY):
-            left = voc_ref[:, t * fw:(t + 1) * fw] if len(voc_ref.shape) == 2 else voc_ref[t]
-            got = dot(left, hid[d, :, t].reshape(NZ * PAD, fw), NT)
-            acc = got if acc is None else acc + got
+    def product(d, t):
+        if len(voc_ref.shape) == 2:
+            start_col = t * fw if isinstance(t, int) else pl.multiple_of(t * fw, 128)
+            left = voc_ref[:, pl.ds(start_col, fw)]
+        else:
+            left = voc_ref[t]
+        return dot(left, hid[d, :, t].reshape(NZ * PAD, fw), NT)
+
+    def finish(d, acc):
         capped = LOGIT_CAP * jnp.tanh(acc * (1.0 / LOGIT_CAP))
         tot = jnp.sum(jnp.exp(capped), axis=0, keepdims=True)
         cho = jnp.sum(jnp.where(vocab_ids == lab_ref[d], capped, 0.0), axis=0, keepdims=True)
@@ -270,24 +329,41 @@
             part[pl.ds(d * per_row + r, 1), :] = tot[:, r * 128:(r + 1) * 128]
             part[pl.ds(R + d * per_row + r, 1), :] = cho[:, r * 128:(r + 1) * 128]
 
+    def logits_of(d):
+        acc = product(d, 0)
+        for t in range(1, NY):
+            acc = acc + product(d, t)
+        finish(d, acc)
+
+    part[2 * R:3 * R, :] = jnp.zeros((R, 128), jnp.float32)
+    part[pl.ds(2 * R + my_block // per_line, 1), :] = code_line
     logits_of(me_d)
     for d in twin:
         for z in range(NZ):
             for t in range(NY):
                 landed(d, z, t)
         logits_of(d)
+    far = [p * NC + 1 - me_c for p in others(me_x, NX)] if NC == 2 else []
+    for i, d in enumerate(x_peers):
+        held[i] = product(d, me_t)
+    for i, d in enumerate(far):
+        for z in range(NZ):
+            landed(d, z, me_t)
+        held[NX - 1 + i] = product(d, me_t)
     for off in offsets:
         guarded(off, lambda z: diagonal(z, start, True))
-    for d in x_peers:
-        logits_of(d)
-    if NC == 2:
-        for p in others(me_x, NX):
-            d = p * NC + 1 - me_c
+    for i, d in enumerate(x_peers):
+        acc = held[i]
+        for t in y_peers:
+            acc = acc + product(d, t)
+        finish(d, acc)
+    for i, d in enumerate(far):
+        acc = held[NX - 1 + i]
+        for t in y_peers:
             for z in range(NZ):
-                for t in range(NY):
-                    landed(d, z, t)
-            logits_of(d)
-    part[2 * R:4 * R, :] = meta_ref[...]
+                landed(d, z, t)
+            acc = acc + product(d, t)
+        finish(d, acc)
 
     def exchange(buf, me, n, sends, recvs, where):
         buf[me] = part[...]
@@ -311,11 +387,17 @@
         exchange(gat_s, me_z, NZ, fs_send, fs_recv, lambda p: dev(z=p)),
     ]
     totals, chosen = part[0:R, :], part[R:2 * R, :]
-    counted, doc = part[2 * R:3 * R, :], part[3 * R:4 * R, :]
+    code = part[2 * R:3 * R, :]
     inside = lax.rem(lax.broadcasted_iota(jnp.int32, (R, 128), 1), PAD) < rows
-    counted = jnp.where(inside, counted, 0.0)
+    counted = jnp.where(inside & (code >= docs), 1.0, 0.0)
+    doc = jnp.where(code >= docs, code - docs, code)
     logprob = jnp.where(inside, counted * (chosen - jnp.log(totals)), 0.0)
-    lp_ref[...] = logprob
+    part[0:R, :] = logprob
+    line = part[pl.ds(my_block // per_line, 1), :]
+    mine = line[:, :rows]
+    for k in range(1, per_line):
+        mine = jnp.where(lax.rem(my_block, per_line) == k, line[:, k * PAD:k * PAD + rows], mine)
+    lp_ref[...] = mine
     names = lax.broadcasted_iota(jnp.int32, (docs, 128), 0).astype(jnp.float32)
     like = jnp.zeros((docs, 128), jnp.float32)
     cnt = jnp.zeros((docs, 128), jnp.float32)
@@ -323,22 +405,23 @@
         hit = names == doc[r:r + 1, :]
         like = like + jnp.where(hit, logprob[r:r + 1, :], 0.0)
         cnt = cnt + jnp.where(hit, counted[r:r + 1, :], 0.0)
-    col = lax.broadcasted_iota(jnp.int32, (docs, 128), 1)
-    docs_ref[...] = jnp.where(
-        col == 0, jnp.sum(like, axis=1, keepdims=True), jnp.sum(cnt, axis=1, keepdims=True)
-    )
+    eye = lax.broadcasted_iota(jnp.int32, (docs, docs), 0) == lax.broadcasted_iota(jnp.int32, (docs, docs), 1)
+    for out, sums in ((like_ref, like), (cnt_ref, cnt)):
+        tall = jnp.sum(sums, axis=1, keepdims=True)
+        out[...] = jnp.sum(jnp.where(eye, tall, 0.0), axis=0, keepdims=True)
 
     def drain(c):
         c.wait_send()
 
-    for s in range(NZ - 1):
-        @pl.when((me_z >= s) & (me_z + 1 < NZ))
-        def _(s=s):
-            for which in range(2):
-                kv_copy(s, which).wait_send()
+    for block in [None, *range(NZ - 1)]:
+        @pl.when((me_z + 1 < NZ) if block is None else (me_z > block) & (me_z + 1 < NZ))
+        def _(block=block):
+            for g in range(groups):
+                for c in kv_copy(block, g):
+                    c.wait_send()
     for i, p in enumerate(others(me_t, NY)):
-        for half in range(2):
-            att_copy(half, p, i).wait_send()
+        for g in range(groups):
+            att_copy(g, p, i).wait_send()
         stat_copy(p, i).wait_send()
     for off in offsets:
         guarded(off, lambda z: column(z, off, drain, False))
@@ -354,29 +437,15 @@
 ):
     ND, NZ, NY = mesh.shape["dp"], mesh.shape["seq"], mesh.shape["tensor"]
     rows = query_vectors.shape[0]
-    seg_row, starts = segment_ids[0], doc_starts[0]
-    seg_count = starts.shape[0]
-    docs = seg_count * ND
-    slots = jnp.arange(seg_count, dtype=jnp.int32)
-    me_d, me_z, me_t = lax.axis_index("dp"), lax.axis_index("seq"), lax.axis_index("tensor")
-    positions = me_z * rows + jnp.arange(rows, dtype=jnp.int32)
-    match = seg_row[:, None] == slots[None, :]
-    doc_first = jnp.sum(jnp.where(match, starts[None, :], 0), axis=1, keepdims=True)
-    ends = jnp.concatenate([starts[1:], jnp.full((1,), rows * NZ, jnp.int32)])
-    doc_end = jnp.sum(jnp.where(match, ends[None, :], 0), axis=1)
-    counted = (positions + 1 < doc_end).astype(jnp.float32)
-    doc_of = jnp.sum(jnp.where(match, doc_index[0][None, :], 0), axis=1).astype(jnp.float32)
+    docs = doc_starts.shape[1] * ND
     blocks = ND * NZ
-    mine = (jnp.arange(blocks)[None, :, None] == me_d * NZ + me_z) & (me_t == 0)
-    facts = jnp.pad(jnp.stack([counted, doc_of]), ((0, 0), (0, PAD - rows)))
-    meta = jnp.where(mine, facts[:, None, :], 0.0).reshape(2 * blocks * PAD // 128, 128)
-    labels = jnp.pad(targets.reshape(ND, NZ, rows), ((0, 0), (0, 0), (0, PAD - rows))).reshape(ND, 1, NZ * PAD)
     fw = out_weight.shape[1]
     voc = vocab_weight
     if fw % 128 != 0:
         voc = voc.reshape(voc.shape[0], NY, fw).transpose(1, 0, 2)
     kvw, qw = key_vectors.shape[1], query_vectors.shape[1]
     heads = qw // HEAD_DIM
+    groups = kvw // HEAD_DIM
     NC = 2 if ND % 2 == 0 else 1
     NX = ND // NC
     R = blocks * PAD // 128
@@ -384,11 +453,13 @@
     dma = pltpu.SemaphoreType.DMA
     vm = pl.BlockSpec(memory_space=pltpu.VMEM)
     anyspace = pl.BlockSpec(memory_space=pl.ANY)
-    logprob, sums = pl.pallas_call(
+    smem = pl.BlockSpec(memory_space=pltpu.SMEM)
+    sums = jax.ShapeDtypeStruct((1, docs), f32)
+    logprob, like, counts = pl.pallas_call(
         functools.partial(body, (ND, NZ, NY, docs)),
-        out_shape=(jax.ShapeDtypeStruct((R, 128), f32), jax.ShapeDtypeStruct((docs, 128), f32)),
-        in_specs=[vm, vm, vm, anyspace, vm, vm, vm, anyspace, vm, vm, vm],
-        out_specs=(vm, vm),
+        out_shape=(jax.ShapeDtypeStruct((1, rows), f32), sums, sums),
+        in_specs=[vm, vm, vm, anyspace, vm, vm, vm, anyspace, vm, smem, smem, vm],
+        out_specs=(vm, vm, vm),
         scratch_shapes=[
             pltpu.VMEM(out_weight.shape, bf16),
             pltpu.VMEM(voc.shape, bf16),
@@ -399,13 +470,15 @@
             pltpu.VMEM((rows, fw), f32),
             pltpu.VMEM((NY, rows, 128), f32),
             pltpu.VMEM((ND, NZ, NY, PAD, fw), bf16),
-            pltpu.VMEM((4 * R, 128), f32),
-            pltpu.VMEM((ND, 4 * R, 128), f32),
-            pltpu.VMEM((NY, 4 * R, 128), f32),
-            pltpu.VMEM((NZ, 4 * R, 128), f32),
+            pltpu.VMEM((ND - NC, voc.shape[-2], NZ * PAD), f32),
+            pltpu.VMEM((ND, 1, NZ * PAD), jnp.int32),
+            pltpu.VMEM((3 * R, 128), f32),
+            pltpu.VMEM((ND, 3 * R, 128), f32),
+            pltpu.VMEM((NY, 3 * R, 128), f32),
+            pltpu.VMEM((NZ, 3 * R, 128), f32),
             dma((2,)),
-            dma((NZ, 2)), dma((NZ, 2)),
-            dma((NY, 2)), dma((NY, 2)),
+            dma((NZ, groups, 2)), dma((NZ, groups, 2)),
+            dma((NY, groups)), dma((NY, groups)),
             dma((NY,)), dma((NY,)),
             dma((ND, NZ, NY)),
             dma((NZ, 2)),
@@ -421,11 +494,10 @@
         ),
         name="packed_loglik",
     )(
-        query_vectors, key_vectors, value_vectors, out_weight, residual, post_gain[None, :],
-        final_gain[None, :], voc, doc_first, labels, meta,
+        query_vectors, key_vectors, value_vectors, out_weight, residual, post_gain, final_gain, voc,
+        segment_ids, doc_starts, doc_index, targets,
     )
-    mine_lp = lax.dynamic_slice_in_dim(logprob.reshape(blocks, PAD), me_d * NZ + me_z, 1, axis=0)
-    return (mine_lp[:, :rows], sums[:, 0], sums[:, 1])
+    return (logprob, like[0], counts[0])
 
 
 def solution(mesh):

time: 89.2 us -> 78.1 us (0.88)
  local copies, waits for them, and re-layouts: 8.89 us -> 3.42 us
  Pallas kernels: 78.1 us -> 73.9 us
  other arithmetic: 0.95 us -> 0 us
    pallas_call x1, Pallas kernels: 78.1 us -> 73.9 us  [local(): pl.pallas_call(functools.partial(body, (ND, NZ, NY, docs)), out_shape=(ja...]
    unnamed x0 -> x3, local copies, waits for them, and re-layouts: none -> 3.42 us
    broadcast_in_dim x3 -> x0, local copies, waits for them, and re-layouts: 3.28 us -> none  [the longest x1 1.29 us: local(): post_gain[None, :]]
    slice x2 -> x0, local copies, waits for them, and re-layouts: 2.22 us -> none  [the longest x1 1.49 us: local(): return (mine_lp[:, :rows], sums[:, 0], sums[:, 1])]
    reshape x3 -> x0, local copies, waits for them, and re-layouts: 2.2 us -> none  [the longest x1 0.77 us: local(): targets.reshape(ND, NZ, rows)]
where the time goes in v2:
time: 78.1 us; the launch traced here: 77.9 us
  Pallas kernels  73.9 us (95%)
  local copies, waits for them, and re-layouts  3.42 us (4%)
    pallas_call x1, Pallas kernels, local(): pl.pallas_call(functools.partial(body, (ND, NZ, NY, docs)), out_shape=(ja...  73.9 us
    unnamed x3, local copies, waits for them, and re-layouts  3.42 us

profile of v2, /device:TPU:0, one launch (start us, length us, event | category | flops | bytes accessed | tf_op | source)
XLA Modules:
  0.0 77.9 jit_solution(3641186465834637422)
XLA Ops:
  0.6 73.9 %packed_loglik.1 = (f32[1,56]{1,0:T(1,128)}, f32[1,32]{1,0:T(1,128)}, f32[1,32]{1,0:T(1,128)}) custom-call(bf16[56,2048]{1,0:T(8,128)(2,1)} %q_ref.1, bf16[56,1024]{1,0:T(8,128)(2,1)} %k_ref.1, bf16[56,1024]{1,0:T(8,128)(2,1)} %v_ref.1, bf16[4096,1792]{1,0:T(8,128)(2,1)} %w_hbm.1, bf16[56,1792]{1,0:T(8,128)(2,1)} %res_ref.1, f32[1792]{0:T(1024)} %pg_ref.1, ...), custom_call_target="tpu_custom_call" | custom-call | tf_op jit(solution)/shard_map/packed_loglik/pallas_call | solution.py:458
  74.5 1.1 %copy.18 = f32[1,56]{1,0:T(1,128)} copy(f32[1,56]{1,0:T(1,128)} %get-tuple-element.12) | data formatting | bytes 448
  75.6 1.1 %copy.19 = f32[32]{0:T(128)} copy(f32[32]{0:T(128)} %bitcast.3) | data formatting | bytes 256
  76.7 1.2 %copy.20 = f32[32]{0:T(128)} copy(f32[32]{0:T(128)} %bitcast.2) | data formatting | bytes 256
